TPU v7x, 256 devices: a whole 4x4x8 slice. The times are simulated.
256 devices in a mesh: row: 16 (over x, y), col: 8 (over z), depth: 2 (over core).
Axes of the slice: x: 4, y: 4, z: 8, core: 2. Of those that a mesh axis runs over, the one named last changes fastest.
Arguments:
- halves: bfloat16 [2, 8192, 16384], P(None, 'row', ('col', 'depth')), may hold values from -6 to 6
- spectrum: float32 [2, 16384], P(None, ('col', 'depth')), as said below
- wanted: int32 [4096], P('col'), may hold values from 0 to 32766, as said below
- fraction: float32 [4096], P('col'), may hold values from 0.05 to 0.95
Outputs:
- eigvec: float32 [2, 8192, 4096], P(None, 'row', ('col', 'depth'))
Inputs may be any that keep to these rules, and one draw needn't show every extreme that they name: Read in the order spectrum[0,0], spectrum[1,0], spectrum[0,1], spectrum[1,1], ... the values rise strictly, each by more than 0.05 over the one before. `wanted`: distinct positions in that merged order of the 32768 eigenvalues.
All inputs are finite; a program needn't handle non-finite values.
Results may differ from a plain program's by a relative error of at most 0.0029.
Values may be sent and summed in bfloat16 or wider, within the bound.
No kernel may reach another device: no remote copies, remote signals or barrier semaphores. Data moves between devices by JAX's collectives and lax.ppermute only.
A program may use at most 128 MiB of HBM per device.

v0:
```python
import functools
import math
import jax
import jax.numpy as jnp
from jax import lax
from jax.sharding import Mesh
from jax.sharding import PartitionSpec as P

ROW = ("row_0", "row_1")


def over_axes(shard, axes):
    return functools.reduce(lax.psum, axes, shard)


def in_one_piece(arrays, axis, dim, along):
    both = jnp.concatenate(arrays, axis=along)
    out, at, done = (lax.all_gather(both, axis, axis=dim, tiled=True), 0, [])
    for a in arrays:
        done.append(lax.slice_in_dim(out, at, at + a.shape[along], axis=along))
        at += a.shape[along]
    return tuple(done)


def cut_along(shard, dim, size):
    shape = shard.shape
    pieces = shard.reshape(*shape[:dim], size, shape[dim] // size, *shape[dim + 1 :])
    return jnp.moveaxis(pieces, dim, 0)


def summed_on_arrival(shard, axis, dim):
    pieces = cut_along(shard, dim, lax.axis_size(axis))
    arrived = lax.all_to_all(pieces, axis, split_axis=0, concat_axis=0, tiled=True)
    return arrived.sum(axis=0)


def root_terms(spectrum_full, wanted):
    ordered = jnp.stack([spectrum_full[0], spectrum_full[1]], axis=1).reshape(-1)
    lower = jnp.take(ordered, wanted)
    upper = jnp.take(ordered, wanted + 1)
    return (lower, upper - lower)


def cauchy_block(seam_part, value_part, lower, width, frac):
    return seam_part[:, :, None] / (
        value_part[:, :, None] - lower[None, None, :] - frac[None, None, :] * width[None, None, :]
    )


def column_norms(seam_full, value_full, lower, width, frac):
    step = seam_full.shape[1] // 8
    total = jnp.zeros(lower.shape, jnp.float32)
    for part in range(8):
        cauchy = cauchy_block(
            seam_full[:, part * step : (part + 1) * step],
            value_full[:, part * step : (part + 1) * step],
            lower,
            width,
            frac,
        )
        total = total + jnp.sum(cauchy * cauchy, axis=(0, 1))
    return jnp.sqrt(total)


def panel_product(piece, seam_part, value_part, lower, width, frac):
    columns = lower.shape[0]
    block = math.gcd(columns, 128)

    def one(index):
        start = index * block
        low = lax.dynamic_slice_in_dim(lower, start, block)
        wid = lax.dynamic_slice_in_dim(width, start, block)
        frc = lax.dynamic_slice_in_dim(frac, start, block)
        cauchy = cauchy_block(seam_part, value_part, low, wid, frc)
        product = jnp.einsum(
            "arh,ahk->ark", piece, cauchy.astype(jnp.bfloat16), preferred_element_type=jnp.float32
        )
        return (product, jnp.zeros((block,), jnp.float32))

    products, sums = lax.map(one, jnp.arange(columns // block))
    product = jnp.transpose(products, (1, 2, 0, 3)).reshape(piece.shape[0], piece.shape[1], columns)
    return (product, sums.reshape(-1))


def body(halves, spectrum, wanted, fraction):
    rows_here = halves.shape[1]
    shard_width = halves.shape[2]
    place = lax.axis_index(ROW)
    low_row = jnp.where(
        place == lax.axis_size(ROW) - 1, halves[0, rows_here - 1].astype(jnp.float32), 0.0
    )
    high_row = jnp.where(place == 0, halves[1, 0].astype(jnp.float32), 0.0)
    seam = over_axes(jnp.stack([low_row, high_row]), ROW)
    seam_full, value_full = in_one_piece((seam, spectrum), ("col", "depth"), 1, 0)
    lower_col, width_col = root_terms(value_full, wanted)
    ncols = lax.axis_size("col")
    ndepth = lax.axis_size("depth")
    layer = lax.axis_index("depth")
    seam_mine = lax.dynamic_index_in_dim(
        seam_full.reshape(2, ncols, ndepth, shard_width), layer, 2, keepdims=False
    ).reshape(2, ncols * shard_width)
    value_mine = lax.dynamic_index_in_dim(
        value_full.reshape(2, ncols, ndepth, shard_width), layer, 2, keepdims=False
    ).reshape(2, ncols * shard_width)
    share = lower_col.shape[0] // ndepth
    product, sums = panel_product(
        lax.all_gather(halves, "col", axis=2, tiled=True),
        seam_mine,
        value_mine,
        lower_col,
        width_col,
        fraction,
    )
    total = product
    product = summed_on_arrival(total, "depth", 2)
    lower_own = lax.dynamic_slice_in_dim(lower_col, layer * share, share)
    width_own = lax.dynamic_slice_in_dim(width_col, layer * share, share)
    frac_own = lax.dynamic_slice_in_dim(fraction, layer * share, share)
    norms = column_norms(seam_full, value_full, lower_own, width_own, frac_own)
    return product / norms[None, None, :]


def solution(mesh):
    split = Mesh(
        mesh.devices.reshape(4, 4, mesh.shape["col"], mesh.shape["depth"]),
        ("row_0", "row_1", "col", "depth"),
    )
    in_specs = (P(None, ROW, ("col", "depth")), P(None, ("col", "depth")), P("col"), P("col"))
    out_specs = P(None, ROW, ("col", "depth"))
    return jax.shard_map(body, mesh=split, in_specs=in_specs, out_specs=out_specs, check_vma=False)
```

profile of v0, /device:TPU:1, one launch (start us, length us, event | category | flops | bytes accessed | tf_op | source)
XLA Modules:
  0.0 244.6 jit_solution(11194111778540224851)
XLA Ops:
  6.5 0.7 all-gather.2.cloned.1.call-update
  7.3 0.7 fusion.7
  8.1 9.4 %psum.14 = f32[2,1024]{1,0:T(2,128)S(1)} all-reduce(f32[2,1024]{1,0:T(2,128)S(1)} %pad_maximum_fusion.2), channel_id=1, replica_groups=mesh['row_0'=4,'row_1'=4,'col'=8,'depth'=2] {'row_0'}, use_global_device_ids=true, to_apply=%region_0.1 | all-reduce | flops 2048 | bytes 16384 | tf_op jit(solution)/shard_map/psum | solution.py:13
  17.5 9.0 %psum.15 = f32[2,1024]{1,0:T(2,128)S(1)} all-reduce(f32[2,1024]{1,0:T(2,128)S(1)} %psum.14), channel_id=1, replica_groups=mesh['row_0'=4,'row_1'=4,'col'=8,'depth'=2] {'row_1'}, use_global_device_ids=true, to_apply=%region_1.2 | all-reduce | flops 2048 | bytes 16384 | tf_op jit(solution)/shard_map/psum | solution.py:13
  26.5 0.7 pad_maximum_fusion.1
  27.2 26.9 %all_gather.6 = f32[4,16384]{1,0:T(4,128)S(1)} all-gather(f32[4,1024]{1,0:T(4,128)S(1)} %pad_maximum_fusion.1), channel_id=1, replica_groups=mesh['row_0'=4,'row_1'=4,'col'=8,'depth'=2] {'col','depth'}, dimensions={1}, use_global_device_ids=true | all-gather | bytes 278528 | tf_op jit(solution)/shard_map/all_gather | solution.py:18
  54.4 5.0 %copy.20 = f32[16384,2]{1,0:T(8,128)} copy(f32[16384,2]{0,1:T(2,128)S(1)} %pad_maximum_fusion) | data formatting | bytes 262144 | tf_op jit(solution)/shard_map/stack | solution.py:38
  59.3 7.0 %reshape.100 = f32[32768]{0:T(1024)S(1)} reshape(f32[16384,2]{1,0:T(8,128)} %copy.20) | data formatting | bytes 262144 | tf_op jit(solution)/shard_map/reshape | solution.py:38
  66.4 3.1 %gather_fusion = f32[512]{0:T(512)S(1)} fusion(f32[32768]{0:T(1024)S(1)} %reshape.100, s32[1024]{0:T(1024)S(1)} %get-tuple-element.109), kind=kCustom, calls=%fused_computation.clone | custom fusion | bytes 6144 | tf_op jit(solution)/shard_map/jit(_take)/gather | solution.py:39
  69.5 3.1 %gather_fusion.1 = f32[512]{0:T(512)S(1)} fusion(f32[32768]{0:T(1024)S(1)} %reshape.100, s32[1024]{0:T(1024)S(1)} %get-tuple-element.108), kind=kCustom, calls=%fused_computation.1.clone | custom fusion | bytes 6144 | tf_op jit(solution)/shard_map/jit(_take)/gather | solution.py:40
  73.6 9.4 %multiply_reduce_fusion.6 = (f32[256]{0:T(256)S(1)}, f32[256]{0:T(256)S(1)}, f32[256]{0:T(256)S(1)}, f32[256]{0:T(256)S(1)}, f32[256]{0:T(256)S(1)}, /*index=5*/f32[256]{0:T(256)S(1)}, f32[256]{0:T(256)S(1)}, f32[256]{0:T(256)S(1)}) fusion(f32[2,2048]{1,0:T(2,128)S(1)} %get-tuple-element.97, f32[2,2048]{1,0:T(2,128)S(1)} %get-tuple-element.98, ...), kind=kLoop, calls=%fused_computation.17 | loop fusion | flops 41940992 | bytes 272384 | tf_op jit(solution)/shard_map/reduce_sum | solution.py:61
  83.0 0.6 add_sqrt_fusion
  83.6 103.3 %all-gather.2.cloned.1.call-done = bf16[2,512,8192]{2,1,0:T(8,128)(2,1)} async-done(((bf16[2,512,1024]{2,1,0:T(8,128)(2,1)}), bf16[2,512,8192]{2,1,0:T(8,128)(2,1)}) %all-gather.2.cloned.1.call-update) | async-done | bytes 16777232 | tf_op jit(solution)/shard_map/all_gather | solution.py:107
  186.9 43.0 %while.10 = (s32[]{:T(128)}, f32[4,2,512,128]{2,3,0,1:T(8,128)S(1)}, f32[2,8,1024]{2,1,0:T(8,128)S(1)}, f32[2,8,1024]{2,1,0:T(8,128)S(1)}, s32[4]{0:T(128)S(1)},...) while((s32[]{:T(128)}, ...), condition=%wide.region_3.5_spmd, body=%wide.region_2.4_spmd.sunk | while | flops 2155872512 | bytes 17698500 | solution.py:80
  186.9 0.6 dynamic_slice.46
  188.3 9.3 %fusion.15 = f32[4,2,512,128]{2,3,0,1:T(8,128)S(1)} fusion(f32[4,2,512,128]{2,3,0,1:T(8,128)S(1)} %get-tuple-element.179, s32[]{:T(128)} %get-tuple-element.178, bf16[2,512,8192]{2,1,0:T(8,128)(2,1)} %get-tuple-element.199, f32[128]{0:T(128)S(1)} %dynamic-slice_multiply_fusion.3, f32[128]{0:T(128)S(1)} %dynamic_slice.47, f32[2,8192]{1,0:T(2,128)S(1)} %bitcast.52, ...), kind=kOutput, calls=%fused_computation.9.clone.1 | convolution fusion | flops 2155872256 | bytes 17433604 | tf_op jit(solution)/shard_map/while/body/eval_jaxpr/arh,ahk->ark/dot_general | solution.py:75
  197.7 0.6 dynamic_slice.46
  199.1 9.3 %fusion.15 = f32[4,2,512,128]{2,3,0,1:T(8,128)S(1)} fusion(f32[4,2,512,128]{2,3,0,1:T(8,128)S(1)} %get-tuple-element.179, s32[]{:T(128)} %get-tuple-element.178, bf16[2,512,8192]{2,1,0:T(8,128)(2,1)} %get-tuple-element.199, f32[128]{0:T(128)S(1)} %dynamic-slice_multiply_fusion.3, f32[128]{0:T(128)S(1)} %dynamic_slice.47, f32[2,8192]{1,0:T(2,128)S(1)} %bitcast.52, ...), kind=kOutput, calls=%fused_computation.9.clone.1 | convolution fusion | flops 2155872256 | bytes 17433604 | tf_op jit(solution)/shard_map/while/body/eval_jaxpr/arh,ahk->ark/dot_general | solution.py:75
  208.4 0.6 dynamic_slice.46
  209.8 9.3 %fusion.15 = f32[4,2,512,128]{2,3,0,1:T(8,128)S(1)} fusion(f32[4,2,512,128]{2,3,0,1:T(8,128)S(1)} %get-tuple-element.179, s32[]{:T(128)} %get-tuple-element.178, bf16[2,512,8192]{2,1,0:T(8,128)(2,1)} %get-tuple-element.199, f32[128]{0:T(128)S(1)} %dynamic-slice_multiply_fusion.3, f32[128]{0:T(128)S(1)} %dynamic_slice.47, f32[2,8192]{1,0:T(2,128)S(1)} %bitcast.52, ...), kind=kOutput, calls=%fused_computation.9.clone.1 | convolution fusion | flops 2155872256 | bytes 17433604 | tf_op jit(solution)/shard_map/while/body/eval_jaxpr/arh,ahk->ark/dot_general | solution.py:75
  219.2 0.6 dynamic_slice.46
  220.6 9.3 %fusion.15 = f32[4,2,512,128]{2,3,0,1:T(8,128)S(1)} fusion(f32[4,2,512,128]{2,3,0,1:T(8,128)S(1)} %get-tuple-element.179, s32[]{:T(128)} %get-tuple-element.178, bf16[2,512,8192]{2,1,0:T(8,128)(2,1)} %get-tuple-element.199, f32[128]{0:T(128)S(1)} %dynamic-slice_multiply_fusion.3, f32[128]{0:T(128)S(1)} %dynamic_slice.47, f32[2,8192]{1,0:T(2,128)S(1)} %bitcast.52, ...), kind=kOutput, calls=%fused_computation.9.clone.1 | convolution fusion | flops 2155872256 | bytes 17433604 | tf_op jit(solution)/shard_map/while/body/eval_jaxpr/arh,ahk->ark/dot_general | solution.py:75
  230.1 5.9 %all_to_all.5 = f32[2,2,512,256]{2,3,1,0:T(8,128)S(1)} all-to-all(f32[2,2,512,256]{2,3,1,0:T(8,128)S(1)} %copy.22), channel_id=1, replica_groups=mesh['row_0'=4,'row_1'=4,'col'=8,'depth'=2] {'depth'}, dimensions={0} | all-to-all | bytes 4194304 | tf_op jit(solution)/shard_map/all_to_all | solution.py:33
  236.5 1.3 copy.24
  (43 shorter events, 2.8 us)
Async XLA Ops:
  6.5 180.4 %all-gather.2.cloned.1.call-start = ((), (), s32[]{:S(2)}) async-start(), calls=%async_computation.1 | async-start | bytes 18874368 | tf_op jit(solution)/shard_map/all_gather | solution.py:107
  59.3 7.0 %copy-start = (s32[512]{0:T(512)S(1)}, s32[512]{0:T(512)}, u32[]{:S(2)}) copy-start(s32[512]{0:T(512)} %param.10) | copy-start | bytes 6148
  66.4 7.1 %copy-start.1 = (f32[512]{0:T(512)S(1)}, f32[512]{0:T(512)}, u32[]{:S(2)}) copy-start(f32[512]{0:T(512)} %param.11) | copy-start | bytes 6148
  230.1 6.2 %copy-start.2 = (f32[256]{0:T(256)S(1)}, f32[256]{0:T(256)}, u32[]{:S(2)}) copy-start(f32[256]{0:T(256)} %add_sqrt_fusion) | copy-start | bytes 3076
Sparse Core Ops, SparseCore 0:
  9.1 177.7 all-gather.1
where the time goes:
time: 245 us
  waiting for transfers between devices  104 us (42%)
  blocking collectives  51.2 us (21%)
  matrix products  37.2 us (15%)
  local copies, waits for them, and re-layouts  23.7 us (10%)
  between operations  13.6 us (6%)
  other arithmetic  12.4 us (5%)
    all_gather x1, waiting for transfers between devices, body(): lax.all_gather(halves, 'col', axis=2, tiled=True)  103 us
    dot_general x4, matrix products, one(): jnp.einsum('arh,ahk->ark', piece, cauchy.astype(jnp.bfloat16), preferred_...  37.2 us
    all_gather x1, blocking collectives, in_one_piece(): out, at, done = (lax.all_gather(both, axis, axis=dim, tiled=True), 0, [])  26.9 us
    psum x2, blocking collectives, over_axes(): return functools.reduce(lax.psum, axes, shard)  18.4 us
    reduce_sum x1, other arithmetic, column_norms(): total = total + jnp.sum(cauchy * cauchy, axis=(0, 1))  9.38 us
    reshape x1, local copies, waits for them, and re-layouts, root_terms(): jnp.stack([spectrum_full[0], spectrum_full[1]], axis=1).reshape(-1)  6.99 us
    all_to_all x1, blocking collectives, summed_on_arrival(): lax.all_to_all(pieces, axis, split_axis=0, concat_axis=0, tiled=True)  5.89 us
    another operation x2, local copies, waits for them, and re-layouts, root_terms(): jnp.stack([spectrum_full[0], spectrum_full[1]], axis=1).reshape(-1)  5.07 us
  transfers between devices with their start and end apart: 1, of which 1 were waited for; matrix products, arithmetic and copies ran while one was open for 13% of the time, Pallas kernels for 0%

commit v1 on v0

--- a/solution.py
+++ b/solution.py
@@ -104,7 +104,9 @@
     ).reshape(2, ncols * shard_width)
     share = lower_col.shape[0] // ndepth
     product, sums = panel_product(
-        lax.all_gather(halves, "col", axis=2, tiled=True),
+        jnp.concatenate(
+            lax.all_to_all(jnp.stack([halves] * lax.axis_size("col")), "col", 0, 0), axis=2
+        ),
         seam_mine,
         value_mine,
         lower_col,

time: 245 us -> 516 us (2.11)
  blocking collectives: 51.2 us -> 380 us
  waiting for transfers between devices: 104 us -> 0.01 us
  local copies, waits for them, and re-layouts: 23.7 us -> 73.2 us
  between operations: 13.6 us -> 0.24 us
  starting transfers between devices: 0.01 us -> 9.13 us
    all_gather x1, blocking collectives: 26.9 us -> 356 us  [in_one_piece(): out, at, done = (lax.all_gather(both, axis, axis=dim, tiled=True), 0, [])]
    all_gather x1 -> x0, waiting for transfers between devices: 103 us -> none  [body(): lax.all_gather(halves, 'col', axis=2, tiled=True)]
    all_to_all x0 -> x1, local copies, waits for them, and re-layouts: none -> 21.8 us  [body(): lax.all_to_all(jnp.stack([halves] * lax.axis_size('col')), 'col', 0, 0)]
    while x8 -> x9, local copies, waits for them, and re-layouts: 0.42 us -> 21.3 us  [the longest x1 20.9 us: panel_product(): products, sums = lax.map(one, jnp.arange(columns // block))]
    all_to_all x0 -> x1, starting transfers between devices: none -> 9.13 us  [body(): lax.all_to_all(jnp.stack([halves] * lax.axis_size('col')), 'col', 0, 0)]
    another operation x0 -> x1, local copies, waits for them, and re-layouts: none -> 6.89 us  [body(): jnp.stack([halves] * lax.axis_size('col'))]
  transfers between devices with their start and end apart: 1 -> 1, of which waited for: 1 -> 0; matrix products, arithmetic and copies ran while one was open for 13% -> 6% of each run, Pallas kernels for 0% -> 0%
where the time goes in v1:
time: 516 us; the launch traced here: 514 us
  blocking collectives  380 us (74%)
  local copies, waits for them, and re-layouts  73.2 us (14%)
  matrix products  37.2 us (7%)
  other arithmetic  11.7 us (2%)
  starting transfers between devices  9.13 us (2%)
    all_gather x1, blocking collectives, in_one_piece(): out, at, done = (lax.all_gather(both, axis, axis=dim, tiled=True), 0, [])  356 us
    dot_general x4, matrix products, one(): jnp.einsum('arh,ahk->ark', piece, cauchy.astype(jnp.bfloat16), preferred_...  37.2 us
    all_to_all x1, local copies, waits for them, and re-layouts, body(): lax.all_to_all(jnp.stack([halves] * lax.axis_size('col')), 'col', 0, 0)  21.8 us
    while x1, local copies, waits for them, and re-layouts, panel_product(): products, sums = lax.map(one, jnp.arange(columns // block))  20.9 us
    psum x2, blocking collectives, over_axes(): return functools.reduce(lax.psum, axes, shard)  18.6 us
  transfers between devices with their start and end apart: 1, of which 0 were waited for; matrix products, arithmetic and copies ran while one was open for 6% of the time, Pallas kernels for 0%

profile of v1, /device:TPU:1, one launch (start us, length us, event | category | flops | bytes accessed | tf_op | source)
XLA Modules:
  0.0 514.1 jit_solution(16635006462776944505)
XLA Ops:
  0.0 6.9 %stack.8 = bf16[8,2,512,1024]{3,2,1,0:T(8,128)(2,1)} broadcast(bf16[2,512,1024]{2,1,0:T(8,128)(2,1)} %param.8), dimensions={1,2,3} | broadcast | bytes 18874368 | tf_op jit(solution)/shard_map/stack | solution.py:108
  6.9 9.1 %all-to-all-start = ((bf16[8,2,512,1024]{3,2,1,0:T(8,128)(2,1)}), bf16[8,2,512,1024]{3,2,1,0:T(8,128)(2,1)}, u32[]{:S(2)}, u32[]{:S(2)}) async-start(bf16[8,2,512,1024]{3,2,1,0:T(8,128)(2,1)} %stack.8), calls=%async_computation | async-start | bytes 33554432 | tf_op jit(solution)/shard_map/all_to_all | solution.py:108
  16.0 0.7 fusion.7
  16.8 9.0 %psum.14 = f32[2,1024]{1,0:T(2,128)S(1)} all-reduce(f32[2,1024]{1,0:T(2,128)S(1)} %pad_maximum_fusion.2), channel_id=1, replica_groups=mesh['row_0'=4,'row_1'=4,'col'=8,'depth'=2] {'row_0'}, use_global_device_ids=true, to_apply=%region_0.1 | all-reduce | flops 2048 | bytes 16384 | tf_op jit(solution)/shard_map/psum | solution.py:13
  25.8 9.6 %psum.15 = f32[2,1024]{1,0:T(2,128)S(1)} all-reduce(f32[2,1024]{1,0:T(2,128)S(1)} %psum.14), channel_id=1, replica_groups=mesh['row_0'=4,'row_1'=4,'col'=8,'depth'=2] {'row_1'}, use_global_device_ids=true, to_apply=%region_1.2 | all-reduce | flops 2048 | bytes 16384 | tf_op jit(solution)/shard_map/psum | solution.py:13
  35.5 356.4 %all_gather.3 = f32[4,16384]{1,0:T(4,128)S(1)} all-gather(f32[4,1024]{1,0:T(4,128)S(1)} %pad_maximum_fusion.1), channel_id=1, replica_groups=mesh['row_0'=4,'row_1'=4,'col'=8,'depth'=2] {'col','depth'}, dimensions={1}, use_global_device_ids=true | all-gather | bytes 278528 | tf_op jit(solution)/shard_map/all_gather | solution.py:18
  392.1 4.9 copy.29
  397.0 6.9 %reshape.108 = f32[32768]{0:T(1024)S(1)} reshape(f32[16384,2]{1,0:T(8,128)} %copy.29) | data formatting | bytes 262144 | tf_op jit(solution)/shard_map/reshape | solution.py:38
  404.0 3.1 gather_fusion
  407.1 3.1 gather_fusion.1
  411.2 9.4 %multiply_reduce_fusion.6 = (f32[256]{0:T(256)S(1)}, f32[256]{0:T(256)S(1)}, f32[256]{0:T(256)S(1)}, f32[256]{0:T(256)S(1)}, f32[256]{0:T(256)S(1)}, /*index=5*/f32[256]{0:T(256)S(1)}, f32[256]{0:T(256)S(1)}, f32[256]{0:T(256)S(1)}) fusion(f32[2,2048]{1,0:T(2,128)S(1)} %get-tuple-element.115, f32[2,2048]{1,0:T(2,128)S(1)} %get-tuple-element.116, ...), kind=kLoop, calls=%fused_computation.17 | loop fusion | flops 41940992 | bytes 272384 | tf_op jit(solution)/shard_map/reduce_sum | solution.py:61
  420.6 0.6 add_sqrt_fusion
  421.2 21.8 %copy.30 = bf16[8,2,512,1024]{2,3,0,1:T(8,128)(2,1)} copy(bf16[8,2,512,1024]{3,2,1,0:T(8,128)(2,1)} %all-to-all-done) | data formatting | bytes 33554432 | tf_op jit(solution)/shard_map/all_to_all | solution.py:108
  443.0 20.9 %copy.31 = bf16[2,512,8192]{2,1,0:T(8,128)(2,1)} copy(bf16[2,512,8192]{1,2,0:T(8,128)(2,1)} %bitcast.50) | data formatting | bytes 33554432 | tf_op jit(solution)/shard_map/while | solution.py:80
  463.9 43.0 %while.10 = (s32[]{:T(128)}, f32[4,2,512,128]{2,3,0,1:T(8,128)S(1)}, f32[2,8,1024]{2,1,0:T(8,128)S(1)}, f32[2,8,1024]{2,1,0:T(8,128)S(1)}, s32[4]{0:T(128)S(1)},...) while((s32[]{:T(128)}, ...), condition=%wide.region_3.5_spmd, body=%wide.region_2.4_spmd.sunk | while | flops 2155872512 | bytes 17698500 | solution.py:80
  465.4 9.3 %fusion.15 = f32[4,2,512,128]{2,3,0,1:T(8,128)S(1)} fusion(f32[4,2,512,128]{2,3,0,1:T(8,128)S(1)} %get-tuple-element.197, s32[]{:T(128)} %get-tuple-element.196, bf16[2,512,8192]{2,1,0:T(8,128)(2,1)} %get-tuple-element.217, f32[128]{0:T(128)S(1)} %dynamic-slice_multiply_fusion.3, f32[128]{0:T(128)S(1)} %dynamic_slice.47, f32[2,8192]{1,0:T(2,128)S(1)} %bitcast.56, ...), kind=kOutput, calls=%fused_computation.9.clone.1 | convolution fusion | flops 2155872256 | bytes 17433604 | tf_op jit(solution)/shard_map/while/body/eval_jaxpr/arh,ahk->ark/dot_general | solution.py:75
  474.7 0.6 dynamic_slice.46
  476.1 9.3 %fusion.15 = f32[4,2,512,128]{2,3,0,1:T(8,128)S(1)} fusion(f32[4,2,512,128]{2,3,0,1:T(8,128)S(1)} %get-tuple-element.197, s32[]{:T(128)} %get-tuple-element.196, bf16[2,512,8192]{2,1,0:T(8,128)(2,1)} %get-tuple-element.217, f32[128]{0:T(128)S(1)} %dynamic-slice_multiply_fusion.3, f32[128]{0:T(128)S(1)} %dynamic_slice.47, f32[2,8192]{1,0:T(2,128)S(1)} %bitcast.56, ...), kind=kOutput, calls=%fused_computation.9.clone.1 | convolution fusion | flops 2155872256 | bytes 17433604 | tf_op jit(solution)/shard_map/while/body/eval_jaxpr/arh,ahk->ark/dot_general | solution.py:75
  485.4 0.6 dynamic_slice.46
  486.9 9.3 %fusion.15 = f32[4,2,512,128]{2,3,0,1:T(8,128)S(1)} fusion(f32[4,2,512,128]{2,3,0,1:T(8,128)S(1)} %get-tuple-element.197, s32[]{:T(128)} %get-tuple-element.196, bf16[2,512,8192]{2,1,0:T(8,128)(2,1)} %get-tuple-element.217, f32[128]{0:T(128)S(1)} %dynamic-slice_multiply_fusion.3, f32[128]{0:T(128)S(1)} %dynamic_slice.47, f32[2,8192]{1,0:T(2,128)S(1)} %bitcast.56, ...), kind=kOutput, calls=%fused_computation.9.clone.1 | convolution fusion | flops 2155872256 | bytes 17433604 | tf_op jit(solution)/shard_map/while/body/eval_jaxpr/arh,ahk->ark/dot_general | solution.py:75
  496.2 0.6 dynamic_slice.46
  497.6 9.3 %fusion.15 = f32[4,2,512,128]{2,3,0,1:T(8,128)S(1)} fusion(f32[4,2,512,128]{2,3,0,1:T(8,128)S(1)} %get-tuple-element.197, s32[]{:T(128)} %get-tuple-element.196, bf16[2,512,8192]{2,1,0:T(8,128)(2,1)} %get-tuple-element.217, f32[128]{0:T(128)S(1)} %dynamic-slice_multiply_fusion.3, f32[128]{0:T(128)S(1)} %dynamic_slice.47, f32[2,8192]{1,0:T(2,128)S(1)} %bitcast.56, ...), kind=kOutput, calls=%fused_computation.9.clone.1 | convolution fusion | flops 2155872256 | bytes 17433604 | tf_op jit(solution)/shard_map/while/body/eval_jaxpr/arh,ahk->ark/dot_general | solution.py:75
  507.1 5.2 %all_to_all.10 = f32[2,2,512,256]{2,3,1,0:T(8,128)S(1)} all-to-all(f32[2,2,512,256]{2,3,1,0:T(8,128)S(1)} %copy.33), channel_id=1, replica_groups=mesh['row_0'=4,'row_1'=4,'col'=8,'depth'=2] {'depth'}, dimensions={0} | all-to-all | bytes 4194304 | tf_op jit(solution)/shard_map/all_to_all | solution.py:33
  512.8 1.3 copy.35
  (47 shorter events, 3.4 us)
Async XLA Ops:
  6.9 28.5 %copy-start.1 = (f32[2,1024]{1,0:T(2,128)S(1)}, f32[2,1024]{1,0:T(2,128)}, u32[]{:S(2)}) copy-start(f32[2,1024]{1,0:T(2,128)} %param.9) | copy-start | bytes 24580
  6.9 414.3 %all-to-all-start = ((bf16[8,2,512,1024]{3,2,1,0:T(8,128)(2,1)}), bf16[8,2,512,1024]{3,2,1,0:T(8,128)(2,1)}, u32[]{:S(2)}, u32[]{:S(2)}) async-start(bf16[8,2,512,1024]{3,2,1,0:T(8,128)(2,1)} %stack.8), calls=%async_computation | async-start | bytes 33554432 | tf_op jit(solution)/shard_map/all_to_all | solution.py:108
  397.0 6.9 %copy-start = (s32[512]{0:T(512)S(1)}, s32[512]{0:T(512)}, u32[]{:S(2)}) copy-start(s32[512]{0:T(512)} %param.10) | copy-start | bytes 6148
  403.9 7.1 %copy-start.2 = (f32[512]{0:T(512)S(1)}, f32[512]{0:T(512)}, u32[]{:S(2)}) copy-start(f32[512]{0:T(512)} %param.11) | copy-start | bytes 6148
  507.1 5.5 %copy-start.3 = (f32[256]{0:T(256)S(1)}, f32[256]{0:T(256)}, u32[]{:S(2)}) copy-start(f32[256]{0:T(256)} %add_sqrt_fusion) | copy-start | bytes 3076
